TPU v7x, 32 devices: a whole 2x2x4 slice. The times are simulated.
32 devices in a mesh: wide: 8 (over z, y), narrow: 4 (over x, core).
Axes of the slice: x: 2, y: 2, z: 4, core: 2. Of those that a mesh axis runs over, the one named last changes fastest.
Arguments:
- queries: bfloat16 [2048, 1024], P(('wide', 'narrow')), may hold values from -16 to 16
- documents: bfloat16 [2048, 1024], P(('wide', 'narrow')), may hold values from -16 to 16
- user_ids: int32 [2048], replicated, may hold values from 0 to 1663, as said below
Outputs:
- query_grad: bfloat16 [2048, 1024], P(('wide', 'narrow'))
- doc_grad: bfloat16 [2048, 1024], P(('wide', 'narrow'))
- loss: float32 [], replicated
Inputs may be any that keep to these rules, and one draw needn't show every extreme that they name: `user_ids`: each user id names at most 4 rows; rows with a common id lie in the same quarter of the 2048 rows.
All inputs are finite; a program needn't handle non-finite values.
Results may differ from a plain program's by a relative error of at most 0.004.
The roundings to bfloat16 on the way count: a program that leaves them out, or rounds other values in their place, can miss the bound.
Values may be sent and summed in bfloat16 or wider, within the bound.
No kernel may reach another device: no remote copies, remote signals or barrier semaphores. Data moves between devices by JAX's collectives and lax.ppermute only.
A program may use at most 64 MiB of HBM per device.

v0:
```python
import math
import jax
import jax.numpy as jnp
from jax import lax
from jax.sharding import PartitionSpec as P


def passed_along(array, axis, by):
    devices = lax.axis_size(axis)
    return lax.ppermute(array, axis, [(i, (i + by) % devices) for i in range(devices)])


def local(queries, documents, user_ids):
    wide_count = lax.axis_size("wide")
    narrow_count = lax.axis_size("narrow")
    own_rows = queries.shape[0]
    width = queries.shape[1]
    wide_index = lax.axis_index("wide")
    narrow_index = lax.axis_index("narrow")
    score_scale = 3.0 / math.sqrt(width)
    batch_rows = jnp.float32(wide_count * narrow_count * own_rows)
    group_queries = lax.all_gather(queries, "narrow", axis=0, tiled=True)
    group_docs = lax.all_gather(documents, "wide", axis=0, tiled=True)
    id_table = user_ids.reshape(wide_count, narrow_count, own_rows)
    query_users = lax.dynamic_index_in_dim(id_table, wide_index, 0, keepdims=False).reshape(-1)
    doc_users = lax.dynamic_index_in_dim(id_table, narrow_index, 1, keepdims=False).reshape(-1)
    positive = query_users[:, None] == doc_users[None, :]
    positive_float = positive.astype(jnp.float32)
    counts_local = jnp.sum(positive_float, axis=1)
    scores = (
        lax.dot_general(
            group_queries, group_docs, (((1,), (1,)), ((), ())), preferred_element_type=jnp.float32
        )
        * score_scale
    )
    pos_local = jnp.sum(jnp.where(positive, scores, jnp.float32(0.0)), axis=1)
    local_peak = jnp.max(scores, axis=1)
    row_peak = lax.pmax(local_peak, "narrow")
    local_denom = jnp.sum(jnp.exp(scores - row_peak[:, None]), axis=1)
    row_denom, counts, pos_sum = lax.psum((local_denom, counts_local, pos_local), "narrow")
    log_denom = row_peak + jnp.log(row_denom)
    row_terms = counts * log_denom - pos_sum
    total, loss_sum = lax.psum((jnp.sum(counts), jnp.sum(row_terms)), "wide")
    probs = jnp.exp(scores - log_denom[:, None])
    weights = (batch_rows * (counts[:, None] * probs - positive_float) / total).astype(jnp.bfloat16)

    def doc_term(first_row, row_count):
        cols_block = lax.dynamic_slice_in_dim(weights, first_row, row_count, 1)
        return (
            lax.dot_general(
                cols_block,
                group_queries,
                (((0,), (0,)), ((), ())),
                preferred_element_type=jnp.float32,
            )
            * score_scale
        )

    query_grad = lax.psum_scatter(
        jnp.dot(weights, group_docs, preferred_element_type=jnp.float32) * score_scale,
        "narrow",
        scatter_dimension=0,
        tiled=True,
    )

    def block_term(block_number):
        start = jnp.mod(block_number, wide_count) * own_rows
        return doc_term(start, own_rows)

    def advance(turn, partial_sum):
        passed = passed_along(partial_sum, "wide", 1)
        return passed + block_term(wide_index - 1 - turn + wide_count)

    doc_grad = lax.fori_loop(1, wide_count, advance, block_term(wide_index - 1 + wide_count))
    return (query_grad.astype(jnp.bfloat16), doc_grad.astype(jnp.bfloat16), loss_sum / total)


def solution(mesh):
    return jax.shard_map(
        local,
        mesh=mesh,
        in_specs=(P(("wide", "narrow"), None), P(("wide", "narrow"), None), P()),
        out_specs=(P(("wide", "narrow"), None), P(("wide", "narrow"), None), P()),
        check_vma=False,
    )
```

profile of v0, /device:TPU:0, one launch (start us, length us, event | category | flops | bytes accessed | tf_op | source)
XLA Modules:
  0.0 175.9 jit_solution(14605701995390080178)
XLA Ops:
  7.2 0.0 copy-start.1
  7.2 0.0 all-gather.2.cloned.1.call-start
  7.2 0.7 all-gather.2.cloned.1.call-update
  7.9 0.0 copy-start.2
  7.9 0.0 reduce-scatter.2.cloned.1.call-start
  8.0 0.6 copy-done.2
  8.6 0.1 reshape.16
  8.7 0.1 eq.26
  8.8 0.1 eq.28
  8.9 0.0 copy-done.1
  8.9 8.6 %all_gather.6 = bf16[256,1024]{1,0:T(8,128)(2,1)S(1)} all-gather(bf16[64,1024]{1,0:T(8,128)(2,1)S(1)} %copy-done.1), channel_id=1, replica_groups=mesh['wide'=8,'narrow'=4] {'narrow'}, dimensions={0}, use_global_device_ids=true | all-gather | bytes 655360 | tf_op jit(solution)/shard_map/all_gather | solution.py:22
  17.5 35.6 %all-gather.2.cloned.1.call-done = bf16[512,1024]{1,0:T(8,128)(2,1)} async-done(((bf16[64,1024]{1,0:T(8,128)(2,1)}), bf16[512,1024]{1,0:T(8,128)(2,1)}) %all-gather.2.cloned.1.call-update) | async-done | bytes 1048592 | tf_op jit(solution)/shard_map/all_gather | solution.py:23
  53.2 1.8 %fusion.9 = (f32[256]{0:T(256)S(1)}, f32[256,512]{1,0:T(8,128)S(1)}) fusion(bf16[256,1024]{1,0:T(8,128)(2,1)S(1)} %all_gather.6, bf16[512,1024]{1,0:T(8,128)(2,1)} %all-gather.2.cloned.1.call-done), kind=kOutput, calls=%fused_computation.21 | convolution fusion | flops 268697344 | bytes 2098176 | tf_op jit(solution)/shard_map/dot_general | solution.py:31
  54.9 0.0 copy-start
  54.9 5.8 %pmax.7 = f32[256]{0:T(256)S(1)} all-reduce(f32[256]{0:T(256)S(1)} %get-tuple-element.161), channel_id=1, replica_groups=mesh['wide'=8,'narrow'=4] {'narrow'}, use_global_device_ids=true, to_apply=%region_3.4 | all-reduce | flops 256 | bytes 2048 | tf_op jit(solution)/shard_map/pmax | solution.py:38
  60.7 0.3 fusion.3
  61.1 6.6 %all-reduce.1 = (f32[256]{0:T(256)S(1)}, f32[256]{0:T(256)S(1)}, f32[256]{0:T(256)S(1)}) all-reduce(f32[256]{0:T(256)S(1)} %get-tuple-element.140, f32[256]{0:T(256)S(1)} %get-tuple-element.142, f32[256]{0:T(256)S(1)} %get-tuple-element.141), channel_id=1, replica_groups=mesh['wide'=8,'narrow'=4] {'narrow'}, use_global_device_ids=true, to_apply=%region_12.13 | all-reduce | flops 768 | bytes 6144 | tf_op jit(solution)/shard_map/psum | solution.py:40
  67.7 0.6 subtract_reduce_fusion
  68.3 19.8 %all-reduce = (f32[]{:T(128)}, f32[]{:T(128)}) all-reduce(f32[]{:T(128)} %get-tuple-element.144, f32[]{:T(128)} %get-tuple-element.143), channel_id=1, replica_groups=mesh['wide'=8,'narrow'=4] {'wide'}, use_global_device_ids=true, to_apply=%region_7.8 | all-reduce | flops 2 | bytes 16 | tf_op jit(solution)/shard_map/psum | solution.py:43
  88.1 0.9 fusion.6
  89.0 0.0 copy-done
  89.0 1.4 convolution_multiply_fusion.1
  90.4 0.0 reduce-scatter.2.cloned.1.call-update
  90.4 0.3 convolution_multiply_fusion.3
  90.8 73.5 %while.15 = (s32[]{:T(128)}, f32[64,1024]{1,0:T(8,128)S(1)}, s32[]{:T(128)}, bf16[256,512]{1,0:T(8,128)(2,1)S(1)}, bf16[256,1024]{1,0:T(8,128)(2,1)S(1)}, /*inde...) while((s32[]{:T(128)}, f32[64,1024]{1,0:T(8,128)S(1)}, s32[]{:T(128)}, ...), condition=%wide.region_10.11_spmd, body=%wide.region_9.10_spmd.sunk | while | flops 33685520 | bytes 2163020 | solution.py:74
  90.8 0.1 collective-permute-start
  90.9 9.2 %collective-permute-done = f32[64,1024]{1,0:T(8,128)S(1)} collective-permute-done((f32[64,1024]{1,0:T(8,128)S(1)}, f32[64,1024]{1,0:T(8,128)S(1)}, u32[]{:S(2)}, u32[]{:S(2)}) %collective-permute-start) | collective-permute-done | bytes 262176 | tf_op jit(solution)/shard_map/while/body/eval_jaxpr/ppermute | solution.py:10
  100.1 0.3 fusion.21
  100.4 0.1 collective-permute-start
  100.5 10.4 %collective-permute-done = f32[64,1024]{1,0:T(8,128)S(1)} collective-permute-done((f32[64,1024]{1,0:T(8,128)S(1)}, f32[64,1024]{1,0:T(8,128)S(1)}, u32[]{:S(2)}, u32[]{:S(2)}) %collective-permute-start) | collective-permute-done | bytes 262176 | tf_op jit(solution)/shard_map/while/body/eval_jaxpr/ppermute | solution.py:10
  110.9 0.3 fusion.21
  111.2 0.1 collective-permute-start
  111.3 11.5 %collective-permute-done = f32[64,1024]{1,0:T(8,128)S(1)} collective-permute-done((f32[64,1024]{1,0:T(8,128)S(1)}, f32[64,1024]{1,0:T(8,128)S(1)}, u32[]{:S(2)}, u32[]{:S(2)}) %collective-permute-start) | collective-permute-done | bytes 262176 | tf_op jit(solution)/shard_map/while/body/eval_jaxpr/ppermute | solution.py:10
  122.8 0.3 fusion.21
  123.2 0.1 collective-permute-start
  123.3 11.0 %collective-permute-done = f32[64,1024]{1,0:T(8,128)S(1)} collective-permute-done((f32[64,1024]{1,0:T(8,128)S(1)}, f32[64,1024]{1,0:T(8,128)S(1)}, u32[]{:S(2)}, u32[]{:S(2)}) %collective-permute-start) | collective-permute-done | bytes 262176 | tf_op jit(solution)/shard_map/while/body/eval_jaxpr/ppermute | solution.py:10
  134.3 0.3 fusion.21
  134.6 0.1 collective-permute-start
  134.7 10.1 %collective-permute-done = f32[64,1024]{1,0:T(8,128)S(1)} collective-permute-done((f32[64,1024]{1,0:T(8,128)S(1)}, f32[64,1024]{1,0:T(8,128)S(1)}, u32[]{:S(2)}, u32[]{:S(2)}) %collective-permute-start) | collective-permute-done | bytes 262176 | tf_op jit(solution)/shard_map/while/body/eval_jaxpr/ppermute | solution.py:10
  144.8 0.3 fusion.21
  145.1 0.1 collective-permute-start
  145.2 9.3 %collective-permute-done = f32[64,1024]{1,0:T(8,128)S(1)} collective-permute-done((f32[64,1024]{1,0:T(8,128)S(1)}, f32[64,1024]{1,0:T(8,128)S(1)}, u32[]{:S(2)}, u32[]{:S(2)}) %collective-permute-start) | collective-permute-done | bytes 262176 | tf_op jit(solution)/shard_map/while/body/eval_jaxpr/ppermute | solution.py:10
  154.5 0.3 fusion.21
  154.8 0.1 collective-permute-start
  154.9 9.0 %collective-permute-done = f32[64,1024]{1,0:T(8,128)S(1)} collective-permute-done((f32[64,1024]{1,0:T(8,128)S(1)}, f32[64,1024]{1,0:T(8,128)S(1)}, u32[]{:S(2)}, u32[]{:S(2)}) %collective-permute-start) | collective-permute-done | bytes 262176 | tf_op jit(solution)/shard_map/while/body/eval_jaxpr/ppermute | solution.py:10
  164.0 0.3 fusion.21
  164.3 0.7 convert_element_type.15
  166.3 0.0 reduce-scatter.2.cloned.1.call-done
  166.3 1.6 convert_element_type.14
  (2 shorter events, 0.0 us)
Async XLA Ops:
  7.2 1.7 copy-start.1
  7.2 46.0 %all-gather.2.cloned.1.call-start = ((), (), s32[]{:S(2)}) async-start(), calls=%async_computation.1 | async-start | bytes 1179648 | tf_op jit(solution)/shard_map/all_gather | solution.py:23
  7.9 0.7 copy-start.2
  7.9 158.4 %reduce-scatter.2.cloned.1.call-start = ((), (), s32[]{:S(2)}) async-start(), calls=%async_computation.2 | async-start | bytes 1310720 | tf_op jit(solution)/shard_map/reduce_scatter | solution.py:59
  54.9 34.0 %copy-start = (bf16[512,1024]{1,0:T(8,128)(2,1)S(1)}, bf16[512,1024]{1,0:T(8,128)(2,1)}, u32[]{:S(2)}) copy-start(bf16[512,1024]{1,0:T(8,128)(2,1)} %all-gather.2.cloned.1.call-done) | copy-start | bytes 3145732
  90.8 9.3 %collective-permute-start = (f32[64,1024]{1,0:T(8,128)S(1)}, f32[64,1024]{1,0:T(8,128)S(1)}, u32[]{:S(2)}, u32[]{:S(2)}) collective-permute-start(f32[64,1024]{1,0:T(8,128)S(1)} %get-tuple-element.206), channel_id=1, source_target_pairs={{0,4},{4,8},{8,12},{12,16},{16,20},{20,24},{24,28},{28,0},{1,5},{5... | collective-permute-start | bytes 786440 | tf_op jit(solution)/shard_map/while/body/eval_jaxpr/ppermute | solution.py:10
  100.4 10.5 %collective-permute-start = (f32[64,1024]{1,0:T(8,128)S(1)}, f32[64,1024]{1,0:T(8,128)S(1)}, u32[]{:S(2)}, u32[]{:S(2)}) collective-permute-start(f32[64,1024]{1,0:T(8,128)S(1)} %get-tuple-element.206), channel_id=1, source_target_pairs={{0,4},{4,8},{8,12},{12,16},{16,20},{20,24},{24,28},{28,0},{1,5},{5... | collective-permute-start | bytes 786440 | tf_op jit(solution)/shard_map/while/body/eval_jaxpr/ppermute | solution.py:10
  111.2 11.6 %collective-permute-start = (f32[64,1024]{1,0:T(8,128)S(1)}, f32[64,1024]{1,0:T(8,128)S(1)}, u32[]{:S(2)}, u32[]{:S(2)}) collective-permute-start(f32[64,1024]{1,0:T(8,128)S(1)} %get-tuple-element.206), channel_id=1, source_target_pairs={{0,4},{4,8},{8,12},{12,16},{16,20},{20,24},{24,28},{28,0},{1,5},{5... | collective-permute-start | bytes 786440 | tf_op jit(solution)/shard_map/while/body/eval_jaxpr/ppermute | solution.py:10
  123.2 11.1 %collective-permute-start = (f32[64,1024]{1,0:T(8,128)S(1)}, f32[64,1024]{1,0:T(8,128)S(1)}, u32[]{:S(2)}, u32[]{:S(2)}) collective-permute-start(f32[64,1024]{1,0:T(8,128)S(1)} %get-tuple-element.206), channel_id=1, source_target_pairs={{0,4},{4,8},{8,12},{12,16},{16,20},{20,24},{24,28},{28,0},{1,5},{5... | collective-permute-start | bytes 786440 | tf_op jit(solution)/shard_map/while/body/eval_jaxpr/ppermute | solution.py:10
  134.6 10.2 %collective-permute-start = (f32[64,1024]{1,0:T(8,128)S(1)}, f32[64,1024]{1,0:T(8,128)S(1)}, u32[]{:S(2)}, u32[]{:S(2)}) collective-permute-start(f32[64,1024]{1,0:T(8,128)S(1)} %get-tuple-element.206), channel_id=1, source_target_pairs={{0,4},{4,8},{8,12},{12,16},{16,20},{20,24},{24,28},{28,0},{1,5},{5... | collective-permute-start | bytes 786440 | tf_op jit(solution)/shard_map/while/body/eval_jaxpr/ppermute | solution.py:10
  145.1 9.4 %collective-permute-start = (f32[64,1024]{1,0:T(8,128)S(1)}, f32[64,1024]{1,0:T(8,128)S(1)}, u32[]{:S(2)}, u32[]{:S(2)}) collective-permute-start(f32[64,1024]{1,0:T(8,128)S(1)} %get-tuple-element.206), channel_id=1, source_target_pairs={{0,4},{4,8},{8,12},{12,16},{16,20},{20,24},{24,28},{28,0},{1,5},{5... | collective-permute-start | bytes 786440 | tf_op jit(solution)/shard_map/while/body/eval_jaxpr/ppermute | solution.py:10
  154.8 9.1 %collective-permute-start = (f32[64,1024]{1,0:T(8,128)S(1)}, f32[64,1024]{1,0:T(8,128)S(1)}, u32[]{:S(2)}, u32[]{:S(2)}) collective-permute-start(f32[64,1024]{1,0:T(8,128)S(1)} %get-tuple-element.206), channel_id=1, source_target_pairs={{0,4},{4,8},{8,12},{12,16},{16,20},{20,24},{24,28},{28,0},{1,5},{5... | collective-permute-start | bytes 786440 | tf_op jit(solution)/shard_map/while/body/eval_jaxpr/ppermute | solution.py:10
Sparse Core Ops, SparseCore 0:
  10.1 42.9 all-gather.1
  90.5 21.4 reduce-scatter.1
where the time goes:
time: 176 us
  waiting for transfers between devices  107 us (61%)
  blocking collectives  40.8 us (23%)
  between operations  16.6 us (9%)
  matrix products  5.65 us (3%)
  other arithmetic  4.13 us (2%)
    ppermute x7, waiting for transfers between devices, passed_along(): lax.ppermute(array, axis, [(i, (i + by) % devices) for i in range(devices)])  70.6 us
    all_gather x1, waiting for transfers between devices, local(): group_docs = lax.all_gather(documents, 'wide', axis=0, tiled=True)  35.6 us
    psum x1, blocking collectives, local(): total, loss_sum = lax.psum((jnp.sum(counts), jnp.sum(row_terms)), 'wide')  19.8 us
    all_gather x1, blocking collectives, local(): group_queries = lax.all_gather(queries, 'narrow', axis=0, tiled=True)  8.63 us
    psum x1, blocking collectives, local(): lax.psum((local_denom, counts_local, pos_local), 'narrow')  6.59 us
    pmax x1, blocking collectives, local(): row_peak = lax.pmax(local_peak, 'narrow')  5.8 us
  transfers between devices with their start and end apart: 9, of which 8 were waited for; matrix products, arithmetic and copies ran while one was open for 2% of the time, Pallas kernels for 0%

commit v1 on v0

--- a/solution.py
+++ b/solution.py
@@ -20,7 +20,12 @@
     score_scale = 3.0 / math.sqrt(width)
     batch_rows = jnp.float32(wide_count * narrow_count * own_rows)
     group_queries = lax.all_gather(queries, "narrow", axis=0, tiled=True)
-    group_docs = lax.all_gather(documents, "wide", axis=0, tiled=True)
+    ring = [documents]
+    for hop in range(7):
+        ring.append(lax.ppermute(ring[-1], "wide", [(dev, (dev + 1) % 8) for dev in range(8)]))
+    group_docs = jnp.roll(
+        jnp.concatenate(ring[::-1], axis=0), (lax.axis_index("wide") + 1) * ring[0].shape[0], axis=0
+    )
     id_table = user_ids.reshape(wide_count, narrow_count, own_rows)
     query_users = lax.dynamic_index_in_dim(id_table, wide_index, 0, keepdims=False).reshape(-1)
     doc_users = lax.dynamic_index_in_dim(id_table, narrow_index, 1, keepdims=False).reshape(-1)

time: 176 us -> 188 us (1.068)
  waiting for transfers between devices: 107 us -> 116 us
  starting transfers between devices: 0.49 us -> 3.51 us
  matrix products: 5.65 us -> 3.62 us
    ppermute x0 -> x7, waiting for transfers between devices: none -> 45.3 us  [local(): lax.ppermute(ring[-1], 'wide', [(dev, (dev + 1) % 8) for dev in range(8)])]
    all_gather x1 -> x0, waiting for transfers between devices: 35.6 us -> none  [local(): group_docs = lax.all_gather(documents, 'wide', axis=0, tiled=True)]
    ppermute x0 -> x7, starting transfers between devices: none -> 3.06 us  [local(): lax.ppermute(ring[-1], 'wide', [(dev, (dev + 1) % 8) for dev in range(8)])]
    psum x1, blocking collectives: 19.8 us -> 22 us  [local(): total, loss_sum = lax.psum((jnp.sum(counts), jnp.sum(row_terms)), 'wide')]
  transfers between devices with their start and end apart: 9 -> 15, of which waited for: 8 -> 13; matrix products, arithmetic and copies ran while one was open for 2% -> 2% of each run, Pallas kernels for 0% -> 0%
where the time goes in v1:
time: 188 us
  waiting for transfers between devices  116 us (62%)
  blocking collectives  42.2 us (22%)
  between operations  16.7 us (9%)
  other arithmetic  3.92 us (2%)
  matrix products  3.62 us (2%)
  starting transfers between devices  3.51 us (2%)
    ppermute x7, waiting for transfers between devices, passed_along(): lax.ppermute(array, axis, [(i, (i + by) % devices) for i in range(devices)])  71.1 us
    ppermute x7, waiting for transfers between devices, local(): lax.ppermute(ring[-1], 'wide', [(dev, (dev + 1) % 8) for dev in range(8)])  45.3 us
    psum x1, blocking collectives, local(): total, loss_sum = lax.psum((jnp.sum(counts), jnp.sum(row_terms)), 'wide')  22 us
    all_gather x1, blocking collectives, local(): group_queries = lax.all_gather(queries, 'narrow', axis=0, tiled=True)  7.7 us
    pmax x1, blocking collectives, local(): row_peak = lax.pmax(local_peak, 'narrow')  6.42 us
    psum x1, blocking collectives, local(): lax.psum((local_denom, counts_local, pos_local), 'narrow')  6.15 us
  transfers between devices with their start and end apart: 15, of which 13 were waited for; matrix products, arithmetic and copies ran while one was open for 2% of the time, Pallas kernels for 0%

profile of v1, /device:TPU:0, one launch (start us, length us, event | category | flops | bytes accessed | tf_op | source)
XLA Modules:
  0.0 188.0 jit_solution(5212989934229001363)
XLA Ops:
  7.2 0.0 copy-start
  7.2 0.0 reduce-scatter.2.cloned.1.call-start
  7.2 3.0 %collective-permute-start.1 = (bf16[64,1024]{1,0:T(8,128)(2,1)}, bf16[64,1024]{1,0:T(8,128)(2,1)S(1)}, u32[]{:S(2)}, u32[]{:S(2)}) collective-permute-start(bf16[64,1024]{1,0:T(8,128)(2,1)} %param.6), channel_id=1, source_target_pairs={{0,4},{4,8},{8,12},{12,16},{16,20},{20,24},{24,28},{28,0},{1,5},{5... | collective-permute-start | bytes 393224 | tf_op jit(solution)/shard_map/ppermute | solution.py:25
  10.3 6.7 %collective-permute-done.1 = bf16[64,1024]{1,0:T(8,128)(2,1)S(1)} collective-permute-done((bf16[64,1024]{1,0:T(8,128)(2,1)}, bf16[64,1024]{1,0:T(8,128)(2,1)S(1)}, u32[]{:S(2)}, u32[]{:S(2)}) %collective-permute-start.1) | collective-permute-done | bytes 131104 | tf_op jit(solution)/shard_map/ppermute | solution.py:25
  17.0 0.0 collective-permute-start.2
  17.0 7.7 %collective-permute-done.2 = bf16[64,1024]{1,0:T(8,128)(2,1)S(1)} collective-permute-done((bf16[64,1024]{1,0:T(8,128)(2,1)S(1)}, bf16[64,1024]{1,0:T(8,128)(2,1)S(1)}, u32[]{:S(2)}, u32[]{:S(2)}) %collective-permute-start.2) | collective-permute-done | bytes 131104 | tf_op jit(solution)/shard_map/ppermute | solution.py:25
  24.7 0.0 collective-permute-start.3
  24.7 7.7 %collective-permute-done.3 = bf16[64,1024]{1,0:T(8,128)(2,1)S(1)} collective-permute-done((bf16[64,1024]{1,0:T(8,128)(2,1)S(1)}, bf16[64,1024]{1,0:T(8,128)(2,1)S(1)}, u32[]{:S(2)}, u32[]{:S(2)}) %collective-permute-start.3) | collective-permute-done | bytes 131104 | tf_op jit(solution)/shard_map/ppermute | solution.py:25
  32.3 0.0 collective-permute-start.4
  32.3 7.7 %collective-permute-done.4 = bf16[64,1024]{1,0:T(8,128)(2,1)S(1)} collective-permute-done((bf16[64,1024]{1,0:T(8,128)(2,1)S(1)}, bf16[64,1024]{1,0:T(8,128)(2,1)S(1)}, u32[]{:S(2)}, u32[]{:S(2)}) %collective-permute-start.4) | collective-permute-done | bytes 131104 | tf_op jit(solution)/shard_map/ppermute | solution.py:25
  40.0 0.0 collective-permute-start.5
  40.0 7.7 %collective-permute-done.5 = bf16[64,1024]{1,0:T(8,128)(2,1)S(1)} collective-permute-done((bf16[64,1024]{1,0:T(8,128)(2,1)S(1)}, bf16[64,1024]{1,0:T(8,128)(2,1)S(1)}, u32[]{:S(2)}, u32[]{:S(2)}) %collective-permute-start.5) | collective-permute-done | bytes 131104 | tf_op jit(solution)/shard_map/ppermute | solution.py:25
  47.7 0.0 collective-permute-start.6
  47.7 0.8 reshape.16
  48.5 0.1 eq.29
  48.6 0.1 eq.31
  48.7 7.9 %collective-permute-done.6 = bf16[64,1024]{1,0:T(8,128)(2,1)S(1)} collective-permute-done((bf16[64,1024]{1,0:T(8,128)(2,1)S(1)}, bf16[64,1024]{1,0:T(8,128)(2,1)S(1)}, u32[]{:S(2)}, u32[]{:S(2)}) %collective-permute-start.6) | collective-permute-done | bytes 131104 | tf_op jit(solution)/shard_map/ppermute | solution.py:25
  56.6 0.0 collective-permute-start.7
  56.6 7.7 %all_gather.3 = bf16[256,1024]{1,0:T(8,128)(2,1)S(1)} all-gather(bf16[64,1024]{1,0:T(8,128)(2,1)} %param.5), channel_id=1, replica_groups=mesh['wide'=8,'narrow'=4] {'narrow'}, dimensions={0}, use_global_device_ids=true | all-gather | bytes 655360 | tf_op jit(solution)/shard_map/all_gather | solution.py:22
  64.3 0.0 collective-permute-done.7
  64.4 0.0 copy-done
  64.6 0.5 fusion.17
  65.1 6.4 %pmax.7 = f32[256]{0:T(256)S(1)} all-reduce(f32[256]{0:T(256)S(1)} %get-tuple-element.166), channel_id=1, replica_groups=mesh['wide'=8,'narrow'=4] {'narrow'}, use_global_device_ids=true, to_apply=%region_3.4 | all-reduce | flops 256 | bytes 2048 | tf_op jit(solution)/shard_map/pmax | solution.py:43
  71.5 0.2 fusion.5
  71.7 6.1 %all-reduce.1 = (f32[256]{0:T(256)S(1)}, f32[256]{0:T(256)S(1)}, f32[256]{0:T(256)S(1)}) all-reduce(f32[256]{0:T(256)S(1)} %get-tuple-element.145, f32[256]{0:T(256)S(1)} %get-tuple-element.147, f32[256]{0:T(256)S(1)} %get-tuple-element.146), channel_id=1, replica_groups=mesh['wide'=8,'narrow'=4] {'narrow'}, use_global_device_ids=true, to_apply=%region_12.13 | all-reduce | flops 768 | bytes 6144 | tf_op jit(solution)/shard_map/psum | solution.py:45
  77.8 0.6 subtract_reduce_fusion
  78.5 22.0 %all-reduce = (f32[]{:T(128)}, f32[]{:T(128)}) all-reduce(f32[]{:T(128)} %get-tuple-element.149, f32[]{:T(128)} %get-tuple-element.148), channel_id=1, replica_groups=mesh['wide'=8,'narrow'=4] {'wide'}, use_global_device_ids=true, to_apply=%region_7.8 | all-reduce | flops 2 | bytes 16 | tf_op jit(solution)/shard_map/psum | solution.py:48
  100.4 0.8 fusion.12
  101.3 1.5 convolution_multiply_fusion.1
  102.7 0.0 reduce-scatter.2.cloned.1.call-update
  104.1 0.2 convolution_multiply_fusion.3
  104.3 73.4 %while.15 = (s32[]{:T(128)}, f32[64,1024]{1,0:T(8,128)S(1)}, s32[]{:T(128)}, bf16[256,512]{0,1:T(8,128)(2,1)S(1)}, bf16[256,1024]{1,0:T(8,128)(2,1)S(1)}, /*inde...) while((s32[]{:T(128)}, f32[64,1024]{1,0:T(8,128)S(1)}, s32[]{:T(128)}, ...), condition=%wide.region_10.11_spmd, body=%wide.region_9.10_spmd.sunk | while | flops 33685520 | bytes 2130252 | solution.py:79
  104.3 0.1 collective-permute-start
  104.4 9.0 %collective-permute-done = f32[64,1024]{1,0:T(8,128)S(1)} collective-permute-done((f32[64,1024]{1,0:T(8,128)S(1)}, f32[64,1024]{1,0:T(8,128)S(1)}, u32[]{:S(2)}, u32[]{:S(2)}) %collective-permute-start) | collective-permute-done | bytes 262176 | tf_op jit(solution)/shard_map/while/body/eval_jaxpr/ppermute | solution.py:10
  113.4 0.2 fusion.27
  113.7 0.1 collective-permute-start
  113.8 9.7 %collective-permute-done = f32[64,1024]{1,0:T(8,128)S(1)} collective-permute-done((f32[64,1024]{1,0:T(8,128)S(1)}, f32[64,1024]{1,0:T(8,128)S(1)}, u32[]{:S(2)}, u32[]{:S(2)}) %collective-permute-start) | collective-permute-done | bytes 262176 | tf_op jit(solution)/shard_map/while/body/eval_jaxpr/ppermute | solution.py:10
  123.4 0.2 fusion.27
  123.6 0.1 collective-permute-start
  123.7 10.8 %collective-permute-done = f32[64,1024]{1,0:T(8,128)S(1)} collective-permute-done((f32[64,1024]{1,0:T(8,128)S(1)}, f32[64,1024]{1,0:T(8,128)S(1)}, u32[]{:S(2)}, u32[]{:S(2)}) %collective-permute-start) | collective-permute-done | bytes 262176 | tf_op jit(solution)/shard_map/while/body/eval_jaxpr/ppermute | solution.py:10
  134.5 0.2 fusion.27
  134.8 0.1 collective-permute-start
  134.9 11.7 %collective-permute-done = f32[64,1024]{1,0:T(8,128)S(1)} collective-permute-done((f32[64,1024]{1,0:T(8,128)S(1)}, f32[64,1024]{1,0:T(8,128)S(1)}, u32[]{:S(2)}, u32[]{:S(2)}) %collective-permute-start) | collective-permute-done | bytes 262176 | tf_op jit(solution)/shard_map/while/body/eval_jaxpr/ppermute | solution.py:10
  146.6 0.2 fusion.27
  146.8 0.1 collective-permute-start
  146.9 10.9 %collective-permute-done = f32[64,1024]{1,0:T(8,128)S(1)} collective-permute-done((f32[64,1024]{1,0:T(8,128)S(1)}, f32[64,1024]{1,0:T(8,128)S(1)}, u32[]{:S(2)}, u32[]{:S(2)}) %collective-permute-start) | collective-permute-done | bytes 262176 | tf_op jit(solution)/shard_map/while/body/eval_jaxpr/ppermute | solution.py:10
  157.8 0.2 fusion.27
  158.0 0.1 collective-permute-start
  158.1 10.0 %collective-permute-done = f32[64,1024]{1,0:T(8,128)S(1)} collective-permute-done((f32[64,1024]{1,0:T(8,128)S(1)}, f32[64,1024]{1,0:T(8,128)S(1)}, u32[]{:S(2)}, u32[]{:S(2)}) %collective-permute-start) | collective-permute-done | bytes 262176 | tf_op jit(solution)/shard_map/while/body/eval_jaxpr/ppermute | solution.py:10
  168.1 0.2 fusion.27
  168.3 0.1 collective-permute-start
  168.4 9.0 %collective-permute-done = f32[64,1024]{1,0:T(8,128)S(1)} collective-permute-done((f32[64,1024]{1,0:T(8,128)S(1)}, f32[64,1024]{1,0:T(8,128)S(1)}, u32[]{:S(2)}, u32[]{:S(2)}) %collective-permute-start) | collective-permute-done | bytes 262176 | tf_op jit(solution)/shard_map/while/body/eval_jaxpr/ppermute | solution.py:10
  177.5 0.2 fusion.27
  177.7 0.7 convert_element_type.15
  178.4 0.0 reduce-scatter.2.cloned.1.call-done
  178.4 1.6 convert_element_type.14
  (18 shorter events, 0.2 us)
Async XLA Ops:
  7.2 57.2 %copy-start = (bf16[64,1024]{1,0:T(8,128)(2,1)S(1)}, bf16[64,1024]{1,0:T(8,128)(2,1)}, u32[]{:S(2)}) copy-start(bf16[64,1024]{1,0:T(8,128)(2,1)} %param.6) | copy-start | bytes 393220
  7.2 171.2 %reduce-scatter.2.cloned.1.call-start = ((), (), s32[]{:S(2)}) async-start(), calls=%async_computation.1 | async-start | bytes 1310720 | tf_op jit(solution)/shard_map/reduce_scatter | solution.py:64
  7.2 9.8 %collective-permute-start.1 = (bf16[64,1024]{1,0:T(8,128)(2,1)}, bf16[64,1024]{1,0:T(8,128)(2,1)S(1)}, u32[]{:S(2)}, u32[]{:S(2)}) collective-permute-start(bf16[64,1024]{1,0:T(8,128)(2,1)} %param.6), channel_id=1, source_target_pairs={{0,4},{4,8},{8,12},{12,16},{16,20},{20,24},{24,28},{28,0},{1,5},{5... | collective-permute-start | bytes 393224 | tf_op jit(solution)/shard_map/ppermute | solution.py:25
  17.0 7.7 %collective-permute-start.2 = (bf16[64,1024]{1,0:T(8,128)(2,1)S(1)}, bf16[64,1024]{1,0:T(8,128)(2,1)S(1)}, u32[]{:S(2)}, u32[]{:S(2)}) collective-permute-start(bf16[64,1024]{1,0:T(8,128)(2,1)S(1)} %collective-permute-done.1), channel_id=1, source_target_pairs={{0,4},{4,8},{8,12},{12,16},{16,20},{20,24},{24,28},{28,0},{1,5},{5... | collective-permute-start | bytes 393224 | tf_op jit(solution)/shard_map/ppermute | solution.py:25
  24.7 7.7 %collective-permute-start.3 = (bf16[64,1024]{1,0:T(8,128)(2,1)S(1)}, bf16[64,1024]{1,0:T(8,128)(2,1)S(1)}, u32[]{:S(2)}, u32[]{:S(2)}) collective-permute-start(bf16[64,1024]{1,0:T(8,128)(2,1)S(1)} %collective-permute-done.2), channel_id=1, source_target_pairs={{0,4},{4,8},{8,12},{12,16},{16,20},{20,24},{24,28},{28,0},{1,5},{5... | collective-permute-start | bytes 393224 | tf_op jit(solution)/shard_map/ppermute | solution.py:25
  32.3 7.7 %collective-permute-start.4 = (bf16[64,1024]{1,0:T(8,128)(2,1)S(1)}, bf16[64,1024]{1,0:T(8,128)(2,1)S(1)}, u32[]{:S(2)}, u32[]{:S(2)}) collective-permute-start(bf16[64,1024]{1,0:T(8,128)(2,1)S(1)} %collective-permute-done.3), channel_id=1, source_target_pairs={{0,4},{4,8},{8,12},{12,16},{16,20},{20,24},{24,28},{28,0},{1,5},{5... | collective-permute-start | bytes 393224 | tf_op jit(solution)/shard_map/ppermute | solution.py:25
  40.0 7.7 %collective-permute-start.5 = (bf16[64,1024]{1,0:T(8,128)(2,1)S(1)}, bf16[64,1024]{1,0:T(8,128)(2,1)S(1)}, u32[]{:S(2)}, u32[]{:S(2)}) collective-permute-start(bf16[64,1024]{1,0:T(8,128)(2,1)S(1)} %collective-permute-done.4), channel_id=1, source_target_pairs={{0,4},{4,8},{8,12},{12,16},{16,20},{20,24},{24,28},{28,0},{1,5},{5... | collective-permute-start | bytes 393224 | tf_op jit(solution)/shard_map/ppermute | solution.py:25
  47.7 8.9 %collective-permute-start.6 = (bf16[64,1024]{1,0:T(8,128)(2,1)S(1)}, bf16[64,1024]{1,0:T(8,128)(2,1)S(1)}, u32[]{:S(2)}, u32[]{:S(2)}) collective-permute-start(bf16[64,1024]{1,0:T(8,128)(2,1)S(1)} %collective-permute-done.5), channel_id=1, source_target_pairs={{0,4},{4,8},{8,12},{12,16},{16,20},{20,24},{24,28},{28,0},{1,5},{5... | collective-permute-start | bytes 393224 | tf_op jit(solution)/shard_map/ppermute | solution.py:25
  56.6 7.7 %collective-permute-start.7 = (bf16[64,1024]{1,0:T(8,128)(2,1)S(1)}, bf16[64,1024]{1,0:T(8,128)(2,1)S(1)}, u32[]{:S(2)}, u32[]{:S(2)}) collective-permute-start(bf16[64,1024]{1,0:T(8,128)(2,1)S(1)} %collective-permute-done.6), channel_id=1, source_target_pairs={{0,4},{4,8},{8,12},{12,16},{16,20},{20,24},{24,28},{28,0},{1,5},{5... | collective-permute-start | bytes 393224 | tf_op jit(solution)/shard_map/ppermute | solution.py:25
  104.3 9.1 %collective-permute-start = (f32[64,1024]{1,0:T(8,128)S(1)}, f32[64,1024]{1,0:T(8,128)S(1)}, u32[]{:S(2)}, u32[]{:S(2)}) collective-permute-start(f32[64,1024]{1,0:T(8,128)S(1)} %get-tuple-element.211), channel_id=1, source_target_pairs={{0,4},{4,8},{8,12},{12,16},{16,20},{20,24},{24,28},{28,0},{1,5},{5... | collective-permute-start | bytes 786440 | tf_op jit(solution)/shard_map/while/body/eval_jaxpr/ppermute | solution.py:10
  113.7 9.7 %collective-permute-start = (f32[64,1024]{1,0:T(8,128)S(1)}, f32[64,1024]{1,0:T(8,128)S(1)}, u32[]{:S(2)}, u32[]{:S(2)}) collective-permute-start(f32[64,1024]{1,0:T(8,128)S(1)} %get-tuple-element.211), channel_id=1, source_target_pairs={{0,4},{4,8},{8,12},{12,16},{16,20},{20,24},{24,28},{28,0},{1,5},{5... | collective-permute-start | bytes 786440 | tf_op jit(solution)/shard_map/while/body/eval_jaxpr/ppermute | solution.py:10
  123.6 10.9 %collective-permute-start = (f32[64,1024]{1,0:T(8,128)S(1)}, f32[64,1024]{1,0:T(8,128)S(1)}, u32[]{:S(2)}, u32[]{:S(2)}) collective-permute-start(f32[64,1024]{1,0:T(8,128)S(1)} %get-tuple-element.211), channel_id=1, source_target_pairs={{0,4},{4,8},{8,12},{12,16},{16,20},{20,24},{24,28},{28,0},{1,5},{5... | collective-permute-start | bytes 786440 | tf_op jit(solution)/shard_map/while/body/eval_jaxpr/ppermute | solution.py:10
  134.8 11.8 %collective-permute-start = (f32[64,1024]{1,0:T(8,128)S(1)}, f32[64,1024]{1,0:T(8,128)S(1)}, u32[]{:S(2)}, u32[]{:S(2)}) collective-permute-start(f32[64,1024]{1,0:T(8,128)S(1)} %get-tuple-element.211), channel_id=1, source_target_pairs={{0,4},{4,8},{8,12},{12,16},{16,20},{20,24},{24,28},{28,0},{1,5},{5... | collective-permute-start | bytes 786440 | tf_op jit(solution)/shard_map/while/body/eval_jaxpr/ppermute | solution.py:10
  146.8 11.0 %collective-permute-start = (f32[64,1024]{1,0:T(8,128)S(1)}, f32[64,1024]{1,0:T(8,128)S(1)}, u32[]{:S(2)}, u32[]{:S(2)}) collective-permute-start(f32[64,1024]{1,0:T(8,128)S(1)} %get-tuple-element.211), channel_id=1, source_target_pairs={{0,4},{4,8},{8,12},{12,16},{16,20},{20,24},{24,28},{28,0},{1,5},{5... | collective-permute-start | bytes 786440 | tf_op jit(solution)/shard_map/while/body/eval_jaxpr/ppermute | solution.py:10
  158.0 10.1 %collective-permute-start = (f32[64,1024]{1,0:T(8,128)S(1)}, f32[64,1024]{1,0:T(8,128)S(1)}, u32[]{:S(2)}, u32[]{:S(2)}) collective-permute-start(f32[64,1024]{1,0:T(8,128)S(1)} %get-tuple-element.211), channel_id=1, source_target_pairs={{0,4},{4,8},{8,12},{12,16},{16,20},{20,24},{24,28},{28,0},{1,5},{5... | collective-permute-start | bytes 786440 | tf_op jit(solution)/shard_map/while/body/eval_jaxpr/ppermute | solution.py:10
  168.3 9.1 %collective-permute-start = (f32[64,1024]{1,0:T(8,128)S(1)}, f32[64,1024]{1,0:T(8,128)S(1)}, u32[]{:S(2)}, u32[]{:S(2)}) collective-permute-start(f32[64,1024]{1,0:T(8,128)S(1)} %get-tuple-element.211), channel_id=1, source_target_pairs={{0,4},{4,8},{8,12},{12,16},{16,20},{20,24},{24,28},{28,0},{1,5},{5... | collective-permute-start | bytes 786440 | tf_op jit(solution)/shard_map/while/body/eval_jaxpr/ppermute | solution.py:10
Sparse Core Ops, SparseCore 0:
  102.9 21.7 reduce-scatter.1
